TPU v7x, 256 devices: a whole 4x4x8 slice. The times are simulated.
256 devices in a mesh: gx: 16 (over x, y), gy: 16 (over z, core).
Axes of the slice: x: 4, y: 4, z: 8, core: 2. Of those that a mesh axis runs over, the one named last changes fastest.
Arguments:
- matrix_tiles: float32 [32, 64, 6, 128, 128], P('gx', 'gy'), may hold values from -4 to 4.5, as said below
- tile_codes: int32 [32, 64, 6], P('gx', 'gy'), may hold values from 0 to 8, as said below
- tile_counts: int32 [32, 64], P('gx', 'gy'), may hold values from 1 to 6, as said below
- right_side: float32 [32, 64, 128], P('gx', 'gy'), may hold values from -8 to 8
- initial_guess: float32 [32, 64, 128], P('gx', 'gy'), may hold values from -4 to 4
Outputs:
- solution: float32 [32, 64, 128], P('gx', 'gy')
- residual: float32 [32, 64, 128], P('gx', 'gy')
- hessenberg: float32 [5, 4], replicated
Inputs may be any that keep to these rules, and one draw needn't show every extreme that they name: tile_codes of slot 0 is 4 (the block itself); the codes of one block row are distinct. `tile_counts`: every block row has at least one live slot; some block row has all 6 slots live. `matrix_tiles`: slot 0 of each block row has a diagonal of 2 to 4 added to its entries.
All inputs are finite; a program needn't handle non-finite values.
Results may differ from a plain program's by a relative error of at most 0.0012.
Values sent between devices are 32-bit elements; how exact they have to be, the bound alone decides.
A program may use at most 64 MiB of HBM per device.

v0:
```python
import jax
import jax.numpy as jnp
from jax import lax
from jax.sharding import Mesh
from jax.sharding import PartitionSpec as P

ITERS = 4
GX = ("gx_0", "gx_1")
GY = ("gy_0", "gy_1")


def extended(cells, sides, width):
    for axis, dim in sides:
        count = lax.axis_size(axis)
        ends = count - 1
        head = lax.slice_in_dim(cells, 0, width, axis=dim)
        tail = lax.slice_in_dim(cells, cells.shape[dim] - width, cells.shape[dim], axis=dim)
        cells = jnp.concatenate(
            [
                lax.ppermute(tail, axis, [(i, (i + 1) % count) for i in range(ends)]),
                cells,
                lax.ppermute(head, axis, [((i + 1) % count, i) for i in range(ends)]),
            ],
            axis=dim,
        )
    return cells


def copy_for_each(value, axis):
    copies = jnp.broadcast_to(value, (lax.axis_size(axis), *value.shape))
    return lax.all_to_all(copies, axis, split_axis=0, concat_axis=0, tiled=True)


def of_everyone(value, axis):
    return copy_for_each(value, axis).sum(axis=0)


def by_axis(value, axes):
    far, near = axes
    nearer = of_everyone(value, near)
    return of_everyone(nearer, far)


def together(arrays, axis):
    line, at, gathered = (jnp.concatenate([a.reshape(-1) for a in arrays]), 0, [])
    running = by_axis(line, axis)
    for a in arrays:
        gathered.append(running[at : at + a.size].reshape(a.shape))
        at += a.size
    return tuple(gathered)


def expand(field):
    widened = extended(field, ((GX, 0),), 1)
    return extended(widened, ((GY, 1),), 1)


def operate(field, matrix_tiles, tile_codes, tile_counts):
    padded = expand(field)
    height, breadth = (tile_codes.shape[0], tile_codes.shape[1])
    stacked = jnp.stack(
        [
            padded[1 + row_step : 1 + row_step + height, 1 + col_step : 1 + col_step + breadth]
            for row_step in (-1, 0, 1)
            for col_step in (-1, 0, 1)
        ]
    )
    present = (
        jnp.arange(tile_codes.shape[2], dtype=jnp.int32)[None, None, :] < tile_counts[:, :, None]
    )
    onehot = (tile_codes[:, :, :, None] == jnp.arange(9, dtype=jnp.int32)) & present[:, :, :, None]
    onehot = onehot.astype(jnp.float32)
    picked = jnp.einsum("xysc,cxyk->xysk", onehot, stacked, precision=lax.Precision.HIGHEST)
    return jnp.einsum("xyskl,xysl->xyk", matrix_tiles, picked, precision=lax.Precision.HIGHEST)


def solve_small(lower, target, steps):
    forward = []
    for row in range(steps):
        total = target[row]
        for column in range(row):
            total = total - lower[row, column] * forward[column]
        forward.append(total / lower[row, row])
    backward = [None] * steps
    for row in reversed(range(steps)):
        total = forward[row]
        for column in range(row + 1, steps):
            total = total - lower[column, row] * backward[column]
        backward[row] = total / lower[row, row]
    return backward


def body(matrix_tiles, tile_codes, tile_counts, right_side, initial_guess):
    start = right_side - operate(initial_guess, matrix_tiles, tile_codes, tile_counts)
    beta = jnp.sqrt(by_axis(jnp.sum(start * start), ("gx_0", ("gx_1", "gy_0", "gy_1"))))
    basis = [start / beta]
    images = []
    hessenberg = jnp.zeros((ITERS + 1, ITERS), jnp.float32)
    for column in range(ITERS):
        vector_new = operate(basis[column], matrix_tiles, tile_codes, tile_counts)
        images.append(vector_new)
        stacked_basis = jnp.stack(basis)
        local_inner = jnp.einsum(
            "jxyk,xyk->j", stacked_basis, vector_new, precision=lax.Precision.HIGHEST
        )
        inners, whole_square = together(
            (local_inner, jnp.sum(vector_new * vector_new)), ("gx_0", ("gx_1", "gy_0", "gy_1"))
        )
        vector_new = vector_new - jnp.einsum(
            "j,jxyk->xyk", inners, stacked_basis, precision=lax.Precision.HIGHEST
        )
        hessenberg = hessenberg.at[: column + 1, column].set(inners)
        length_new = jnp.sqrt(whole_square - jnp.sum(inners * inners))
        hessenberg = hessenberg.at[column + 1, column].set(length_new)
        if column + 1 < ITERS:
            basis.append(vector_new / length_new)
    normal_matrix = jnp.dot(hessenberg.T, hessenberg, precision=lax.Precision.HIGHEST)
    target = beta * hessenberg[0, :]
    lower = jnp.linalg.cholesky(normal_matrix)
    weights = solve_small(lower, target, ITERS)
    solution = initial_guess
    for column in range(ITERS):
        solution = solution + weights[column] * basis[column]
    residual = start
    for column in range(ITERS):
        residual = residual - weights[column] * images[column]
    return (solution, residual, hessenberg)


def solution(mesh):
    torus = Mesh(mesh.devices.reshape(4, 4, 8, 2), ("gx_0", "gx_1", "gy_0", "gy_1"))
    in_specs = (
        P(GX, GY, None, None, None),
        P(GX, GY, None),
        P(GX, GY),
        P(GX, GY, None),
        P(GX, GY, None),
    )
    out_specs = (P(GX, GY, None), P(GX, GY, None), P())
    return jax.shard_map(body, mesh=torus, in_specs=in_specs, out_specs=out_specs, check_vma=False)
```

profile of v0, /device:TPU:1, one launch (start us, length us, event | category | flops | bytes accessed | tf_op | source)
XLA Modules:
  0.0 278.9 jit_solution(10043535636046016764)
XLA Ops:
  1.5 4.1 %collective-permute-start = (f32[1,4,128]{2,1,0:T(4,128)S(1)}, f32[1,4,128]{2,1,0:T(4,128)S(1)}, u32[]{:S(2)}, u32[]{:S(2)}) collective-permute-start(f32[1,4,128]{2,1,0:T(4,128)S(1)} %get-tuple-element.140), channel_id=1, source_target_pairs={{0,16},{16,32},{32,48},{48,64},{64,80},{80,96},{96,112},{112,128},... | collective-permute-start | bytes 6152 | tf_op jit(solution)/shard_map/ppermute | solution.py:20
  7.0 3.0 %collective-permute-done.1 = f32[1,4,128]{2,1,0:T(4,128)S(1)} collective-permute-done((f32[1,4,128]{2,1,0:T(4,128)S(1)}, f32[1,4,128]{2,1,0:T(4,128)S(1)}, u32[]{:S(2)}, u32[]{:S(2)}) %collective-permute-start.1) | collective-permute-done | bytes 2080 | tf_op jit(solution)/shard_map/ppermute | solution.py:22
  10.8 4.0 %collective-permute-start.3 = (f32[4,1,128]{2,1,0:T(1,128)S(1)}, f32[4,1,128]{2,1,0:T(1,128)S(1)}, u32[]{:S(2)}, u32[]{:S(2)}) collective-permute-start(f32[4,1,128]{2,1,0:T(1,128)S(1)} %get-tuple-element.124), channel_id=1, source_target_pairs={{1,0},{2,1},{3,2},{4,3},{5,4},{6,5},{7,6},{8,7},{9,8},{10,9},{11,1... | collective-permute-start | bytes 6152 | tf_op jit(solution)/shard_map/ppermute | solution.py:22
  14.8 3.4 %collective-permute-start.2 = (f32[4,1,128]{2,1,0:T(1,128)S(1)}, f32[4,1,128]{2,1,0:T(1,128)S(1)}, u32[]{:S(2)}, u32[]{:S(2)}) collective-permute-start(f32[4,1,128]{2,1,0:T(1,128)S(1)} %get-tuple-element.125), channel_id=1, source_target_pairs={{0,1},{1,2},{2,3},{3,4},{4,5},{5,6},{6,7},{7,8},{8,9},{9,10},{10,1... | collective-permute-start | bytes 6152 | tf_op jit(solution)/shard_map/ppermute | solution.py:20
  25.3 15.1 %all-to-all-start = ((f32[64,1,1]{2,1,0:T(1,128)}), f32[64,1,1]{2,1,0:T(1,128)S(1)}, u32[]{:S(2)}, u32[]{:S(2)}) async-start(f32[64,1,1]{2,1,0:T(1,128)} %broadcast_in_dim.20), calls=%async_computation | async-start | bytes 65536 | tf_op jit(solution)/shard_map/all_to_all | solution.py:31
  41.1 8.6 %all-to-all-done = f32[64,1,1]{2,1,0:T(1,128)S(1)} async-done(((f32[64,1,1]{2,1,0:T(1,128)}), f32[64,1,1]{2,1,0:T(1,128)S(1)}, u32[]{:S(2)}, u32[]{:S(2)}) %all-to-all-start) | async-done | bytes 288 | tf_op jit(solution)/shard_map/all_to_all | solution.py:31
  51.0 7.7 %all_to_all.60 = f32[4,1,1]{2,1,0:T(1,128)S(1)} all-to-all(f32[4,1,1]{2,1,0:T(1,128)S(1)} %broadcast_in_dim.21), channel_id=1, replica_groups=mesh['gx_0'=4,'gx_1'=4,'gy_0'=8,'gy_1'=2] {'gx_0'}, dimensions={0} | all-to-all | bytes 32 | tf_op jit(solution)/shard_map/all_to_all | solution.py:31
  61.3 4.0 %collective-permute-start.4 = (f32[1,4,128]{2,1,0:T(4,128)S(1)}, f32[1,4,128]{2,1,0:T(4,128)S(1)}, u32[]{:S(2)}, u32[]{:S(2)}) collective-permute-start(f32[1,4,128]{2,1,0:T(4,128)S(1)} %get-tuple-element.134), channel_id=1, source_target_pairs={{0,16},{16,32},{32,48},{48,64},{64,80},{80,96},{96,112},{112,128},... | collective-permute-start | bytes 6152 | tf_op jit(solution)/shard_map/ppermute | solution.py:20
  66.0 5.4 %collective-permute-start.6 = (f32[4,1,128]{2,1,0:T(1,128)S(1)}, f32[4,1,128]{2,1,0:T(1,128)S(1)}, u32[]{:S(2)}, u32[]{:S(2)}) collective-permute-start(f32[4,1,128]{2,1,0:T(1,128)S(1)} %get-tuple-element.120), channel_id=1, source_target_pairs={{0,1},{1,2},{2,3},{3,4},{4,5},{5,6},{6,7},{7,8},{8,9},{9,10},{10,1... | collective-permute-start | bytes 6152 | tf_op jit(solution)/shard_map/ppermute | solution.py:20
  73.9 2.9 %collective-permute-done.7 = f32[4,1,128]{2,1,0:T(1,128)S(1)} collective-permute-done((f32[4,1,128]{2,1,0:T(1,128)S(1)}, f32[4,1,128]{2,1,0:T(1,128)S(1)}, u32[]{:S(2)}, u32[]{:S(2)}) %collective-permute-start.7) | collective-permute-done | bytes 2080 | tf_op jit(solution)/shard_map/ppermute | solution.py:22
  83.1 6.5 %all-to-all-start.2 = ((f32[64,1,2]{2,1,0:T(1,128)}), f32[64,1,2]{2,1,0:T(1,128)S(1)}, u32[]{:S(2)}, u32[]{:S(2)}) async-start(f32[64,1,2]{2,1,0:T(1,128)} %broadcast_in_dim.22), calls=%async_computation.2 | async-start | bytes 65536 | tf_op jit(solution)/shard_map/all_to_all | solution.py:31
  89.6 9.3 %all-to-all-done.2 = f32[64,1,2]{2,1,0:T(1,128)S(1)} async-done(((f32[64,1,2]{2,1,0:T(1,128)}), f32[64,1,2]{2,1,0:T(1,128)S(1)}, u32[]{:S(2)}, u32[]{:S(2)}) %all-to-all-start.2) | async-done | bytes 544 | tf_op jit(solution)/shard_map/all_to_all | solution.py:31
  99.0 7.8 %all_to_all.61 = f32[4,1,2]{2,1,0:T(1,128)S(1)} all-to-all(f32[4,1,2]{2,1,0:T(1,128)S(1)} %broadcast_in_dim.23), channel_id=1, replica_groups=mesh['gx_0'=4,'gx_1'=4,'gy_0'=8,'gy_1'=2] {'gx_0'}, dimensions={0} | all-to-all | bytes 64 | tf_op jit(solution)/shard_map/all_to_all | solution.py:31
  111.4 4.0 %collective-permute-start.8 = (f32[1,4,128]{2,1,0:T(4,128)S(1)}, f32[1,4,128]{2,1,0:T(4,128)S(1)}, u32[]{:S(2)}, u32[]{:S(2)}) collective-permute-start(f32[1,4,128]{2,1,0:T(4,128)S(1)} %get-tuple-element.132), channel_id=1, source_target_pairs={{0,16},{16,32},{32,48},{48,64},{64,80},{80,96},{96,112},{112,128},... | collective-permute-start | bytes 6152 | tf_op jit(solution)/shard_map/ppermute | solution.py:20
  116.1 5.4 %collective-permute-start.10 = (f32[4,1,128]{2,1,0:T(1,128)S(1)}, f32[4,1,128]{2,1,0:T(1,128)S(1)}, u32[]{:S(2)}, u32[]{:S(2)}) collective-permute-start(f32[4,1,128]{2,1,0:T(1,128)S(1)} %get-tuple-element.118), channel_id=1, source_target_pairs={{0,1},{1,2},{2,3},{3,4},{4,5},{5,6},{6,7},{7,8},{8,9},{9,10},{10,1... | collective-permute-start | bytes 6152 | tf_op jit(solution)/shard_map/ppermute | solution.py:20
  123.5 2.9 %collective-permute-done.11 = f32[4,1,128]{2,1,0:T(1,128)S(1)} collective-permute-done((f32[4,1,128]{2,1,0:T(1,128)S(1)}, f32[4,1,128]{2,1,0:T(1,128)S(1)}, u32[]{:S(2)}, u32[]{:S(2)}) %collective-permute-start.11) | collective-permute-done | bytes 2080 | tf_op jit(solution)/shard_map/ppermute | solution.py:22
  131.6 6.5 %all-to-all-start.4 = ((f32[64,1,3]{2,1,0:T(1,128)}), f32[64,1,3]{2,1,0:T(1,128)S(1)}, u32[]{:S(2)}, u32[]{:S(2)}) async-start(f32[64,1,3]{2,1,0:T(1,128)} %broadcast_in_dim.24), calls=%async_computation.4 | async-start | bytes 65536 | tf_op jit(solution)/shard_map/all_to_all | solution.py:31
  138.7 8.7 %all-to-all-done.4 = f32[64,1,3]{2,1,0:T(1,128)S(1)} async-done(((f32[64,1,3]{2,1,0:T(1,128)}), f32[64,1,3]{2,1,0:T(1,128)S(1)}, u32[]{:S(2)}, u32[]{:S(2)}) %all-to-all-start.4) | async-done | bytes 800 | tf_op jit(solution)/shard_map/all_to_all | solution.py:31
  147.5 7.8 %all_to_all.62 = f32[4,1,3]{2,1,0:T(1,128)S(1)} all-to-all(f32[4,1,3]{2,1,0:T(1,128)S(1)} %broadcast_in_dim.25), channel_id=1, replica_groups=mesh['gx_0'=4,'gx_1'=4,'gy_0'=8,'gy_1'=2] {'gx_0'}, dimensions={0} | all-to-all | bytes 96 | tf_op jit(solution)/shard_map/all_to_all | solution.py:31
  159.5 4.0 %collective-permute-start.12 = (f32[1,4,128]{2,1,0:T(4,128)S(1)}, f32[1,4,128]{2,1,0:T(4,128)S(1)}, u32[]{:S(2)}, u32[]{:S(2)}) collective-permute-start(f32[1,4,128]{2,1,0:T(4,128)S(1)} %get-tuple-element.130), channel_id=1, source_target_pairs={{0,16},{16,32},{32,48},{48,64},{64,80},{80,96},{96,112},{112,128},... | collective-permute-start | bytes 6152 | tf_op jit(solution)/shard_map/ppermute | solution.py:20
  164.2 5.4 %collective-permute-start.14 = (f32[4,1,128]{2,1,0:T(1,128)S(1)}, f32[4,1,128]{2,1,0:T(1,128)S(1)}, u32[]{:S(2)}, u32[]{:S(2)}) collective-permute-start(f32[4,1,128]{2,1,0:T(1,128)S(1)} %get-tuple-element.116), channel_id=1, source_target_pairs={{0,1},{1,2},{2,3},{3,4},{4,5},{5,6},{6,7},{7,8},{8,9},{9,10},{10,1... | collective-permute-start | bytes 6152 | tf_op jit(solution)/shard_map/ppermute | solution.py:20
  171.5 2.9 %collective-permute-done.15 = f32[4,1,128]{2,1,0:T(1,128)S(1)} collective-permute-done((f32[4,1,128]{2,1,0:T(1,128)S(1)}, f32[4,1,128]{2,1,0:T(1,128)S(1)}, u32[]{:S(2)}, u32[]{:S(2)}) %collective-permute-start.15) | collective-permute-done | bytes 2080 | tf_op jit(solution)/shard_map/ppermute | solution.py:22
  179.8 6.5 %all-to-all-start.6 = ((f32[64,1,4]{2,1,0:T(1,128)}), f32[64,1,4]{2,1,0:T(1,128)S(1)}, u32[]{:S(2)}, u32[]{:S(2)}) async-start(f32[64,1,4]{2,1,0:T(1,128)} %broadcast_in_dim.26), calls=%async_computation.6 | async-start | bytes 65536 | tf_op jit(solution)/shard_map/all_to_all | solution.py:31
  188.3 7.3 %all-to-all-done.6 = f32[64,1,4]{2,1,0:T(1,128)S(1)} async-done(((f32[64,1,4]{2,1,0:T(1,128)}), f32[64,1,4]{2,1,0:T(1,128)S(1)}, u32[]{:S(2)}, u32[]{:S(2)}) %all-to-all-start.6) | async-done | bytes 1056 | tf_op jit(solution)/shard_map/all_to_all | solution.py:31
  195.7 7.8 %all_to_all.63 = f32[4,1,4]{2,1,0:T(1,128)S(1)} all-to-all(f32[4,1,4]{2,1,0:T(1,128)S(1)} %broadcast_in_dim.27), channel_id=1, replica_groups=mesh['gx_0'=4,'gx_1'=4,'gy_0'=8,'gy_1'=2] {'gx_0'}, dimensions={0} | all-to-all | bytes 128 | tf_op jit(solution)/shard_map/all_to_all | solution.py:31
  207.5 4.0 %collective-permute-start.16 = (f32[1,4,128]{2,1,0:T(4,128)S(1)}, f32[1,4,128]{2,1,0:T(4,128)S(1)}, u32[]{:S(2)}, u32[]{:S(2)}) collective-permute-start(f32[1,4,128]{2,1,0:T(4,128)S(1)} %get-tuple-element.128), channel_id=1, source_target_pairs={{0,16},{16,32},{32,48},{48,64},{64,80},{80,96},{96,112},{112,128},... | collective-permute-start | bytes 6152 | tf_op jit(solution)/shard_map/ppermute | solution.py:20
  215.0 4.8 %collective-permute-start.18 = (f32[4,1,128]{2,1,0:T(1,128)S(1)}, f32[4,1,128]{2,1,0:T(1,128)S(1)}, u32[]{:S(2)}, u32[]{:S(2)}) collective-permute-start(f32[4,1,128]{2,1,0:T(1,128)S(1)} %get-tuple-element.114), channel_id=1, source_target_pairs={{0,1},{1,2},{2,3},{3,4},{4,5},{5,6},{6,7},{7,8},{8,9},{9,10},{10,1... | collective-permute-start | bytes 6152 | tf_op jit(solution)/shard_map/ppermute | solution.py:20
  221.8 2.9 %collective-permute-done.19 = f32[4,1,128]{2,1,0:T(1,128)S(1)} collective-permute-done((f32[4,1,128]{2,1,0:T(1,128)S(1)}, f32[4,1,128]{2,1,0:T(1,128)S(1)}, u32[]{:S(2)}, u32[]{:S(2)}) %collective-permute-start.19) | collective-permute-done | bytes 2080 | tf_op jit(solution)/shard_map/ppermute | solution.py:22
  229.9 6.5 %all-to-all-start.8 = ((f32[64,1,5]{2,1,0:T(1,128)}), f32[64,1,5]{2,1,0:T(1,128)S(1)}, u32[]{:S(2)}, u32[]{:S(2)}) async-start(f32[64,1,5]{2,1,0:T(1,128)} %broadcast_in_dim.28), calls=%async_computation.8 | async-start | bytes 65536 | tf_op jit(solution)/shard_map/all_to_all | solution.py:31
  239.8 6.0 %all-to-all-done.8 = f32[64,1,5]{2,1,0:T(1,128)S(1)} async-done(((f32[64,1,5]{2,1,0:T(1,128)}), f32[64,1,5]{2,1,0:T(1,128)S(1)}, u32[]{:S(2)}, u32[]{:S(2)}) %all-to-all-start.8) | async-done | bytes 1312 | tf_op jit(solution)/shard_map/all_to_all | solution.py:31
  246.4 3.2 %all-to-all-start.9 = ((f32[4,1,5]{2,1,0:T(1,128)}), f32[4,1,5]{2,1,0:T(1,128)S(1)}, u32[]{:S(2)}, u32[]{:S(2)}) async-start(f32[4,1,5]{2,1,0:T(1,128)} %broadcast_in_dim.29), calls=%async_computation.9 | async-start | bytes 4096 | tf_op jit(solution)/shard_map/all_to_all | solution.py:31
  249.7 3.9 %all-to-all-done.9 = f32[4,1,5]{2,1,0:T(1,128)S(1)} async-done(((f32[4,1,5]{2,1,0:T(1,128)}), f32[4,1,5]{2,1,0:T(1,128)S(1)}, u32[]{:S(2)}, u32[]{:S(2)}) %all-to-all-start.9) | async-done | bytes 112 | tf_op jit(solution)/shard_map/all_to_all | solution.py:31
  (175 shorter events, 73.1 us)
Async XLA Ops:
  0.6 20.1 %copy-start = (f32[2,4,6,128,128]{4,3,2,1,0:T(8,128)S(1)}, f32[2,4,6,128,128]{4,3,2,1,0:T(8,128)}, u32[]{:S(2)}) copy-start(f32[2,4,6,128,128]{4,3,2,1,0:T(8,128)} %param.21) | copy-start | bytes 9437188
  0.6 39.7 %copy-start.6 = (s32[2]{0:T(128)S(1)}, s32[2]{0:T(128)}, u32[]{:S(2)}) copy-start(s32[2]{0:T(128)} %constant.240.clone.1) | copy-start | bytes 28
  0.7 64.6 %copy-start.5 = (s32[2]{0:T(128)S(1)}, s32[2]{0:T(128)}, u32[]{:S(2)}) copy-start(s32[2]{0:T(128)} %constant.241.clone.1) | copy-start | bytes 28
  0.7 76.3 %copy-start.4 = (s32[2,4,6]{2,1,0:T(4,128)S(1)}, s32[2,4,6]{2,1,0:T(4,128)}, u32[]{:S(2)}) copy-start(s32[2,4,6]{2,1,0:T(4,128)} %param.22) | copy-start | bytes 580
  0.7 22.7 %copy-start.3 = (f32[2,4,128]{2,1,0:T(4,128)S(1)}, f32[2,4,128]{2,1,0:T(4,128)}, u32[]{:S(2)}) copy-start(f32[2,4,128]{2,1,0:T(4,128)} %param.24) | copy-start | bytes 12292
  1.5 5.4 %collective-permute-start = (f32[1,4,128]{2,1,0:T(4,128)S(1)}, f32[1,4,128]{2,1,0:T(4,128)S(1)}, u32[]{:S(2)}, u32[]{:S(2)}) collective-permute-start(f32[1,4,128]{2,1,0:T(4,128)S(1)} %get-tuple-element.140), channel_id=1, source_target_pairs={{0,16},{16,32},{32,48},{48,64},{64,80},{80,96},{96,112},{112,128},... | collective-permute-start | bytes 6152 | tf_op jit(solution)/shard_map/ppermute | solution.py:20
  5.7 4.3 %collective-permute-start.1 = (f32[1,4,128]{2,1,0:T(4,128)S(1)}, f32[1,4,128]{2,1,0:T(4,128)S(1)}, u32[]{:S(2)}, u32[]{:S(2)}) collective-permute-start(f32[1,4,128]{2,1,0:T(4,128)S(1)} %get-tuple-element.139), channel_id=1, source_target_pairs={{16,0},{32,16},{48,32},{64,48},{80,64},{96,80},{112,96},{128,112},... | collective-permute-start | bytes 6152 | tf_op jit(solution)/shard_map/ppermute | solution.py:22
  10.8 8.2 %collective-permute-start.3 = (f32[4,1,128]{2,1,0:T(1,128)S(1)}, f32[4,1,128]{2,1,0:T(1,128)S(1)}, u32[]{:S(2)}, u32[]{:S(2)}) collective-permute-start(f32[4,1,128]{2,1,0:T(1,128)S(1)} %get-tuple-element.124), channel_id=1, source_target_pairs={{1,0},{2,1},{3,2},{4,3},{5,4},{6,5},{7,6},{8,7},{9,8},{10,9},{11,1... | collective-permute-start | bytes 6152 | tf_op jit(solution)/shard_map/ppermute | solution.py:22
  14.8 4.2 %collective-permute-start.2 = (f32[4,1,128]{2,1,0:T(1,128)S(1)}, f32[4,1,128]{2,1,0:T(1,128)S(1)}, u32[]{:S(2)}, u32[]{:S(2)}) collective-permute-start(f32[4,1,128]{2,1,0:T(1,128)S(1)} %get-tuple-element.125), channel_id=1, source_target_pairs={{0,1},{1,2},{2,3},{3,4},{4,5},{5,6},{6,7},{7,8},{8,9},{9,10},{10,1... | collective-permute-start | bytes 6152 | tf_op jit(solution)/shard_map/ppermute | solution.py:20
  25.3 24.4 %all-to-all-start = ((f32[64,1,1]{2,1,0:T(1,128)}), f32[64,1,1]{2,1,0:T(1,128)S(1)}, u32[]{:S(2)}, u32[]{:S(2)}) async-start(f32[64,1,1]{2,1,0:T(1,128)} %broadcast_in_dim.20), calls=%async_computation | async-start | bytes 65536 | tf_op jit(solution)/shard_map/all_to_all | solution.py:31
  60.0 6.0 %collective-permute-start.5 = (f32[1,4,128]{2,1,0:T(4,128)S(1)}, f32[1,4,128]{2,1,0:T(4,128)S(1)}, u32[]{:S(2)}, u32[]{:S(2)}) collective-permute-start(f32[1,4,128]{2,1,0:T(4,128)S(1)} %get-tuple-element.135), channel_id=1, source_target_pairs={{16,0},{32,16},{48,32},{64,48},{80,64},{96,80},{112,96},{128,112},... | collective-permute-start | bytes 6152 | tf_op jit(solution)/shard_map/ppermute | solution.py:22
  61.3 4.7 %collective-permute-start.4 = (f32[1,4,128]{2,1,0:T(4,128)S(1)}, f32[1,4,128]{2,1,0:T(4,128)S(1)}, u32[]{:S(2)}, u32[]{:S(2)}) collective-permute-start(f32[1,4,128]{2,1,0:T(4,128)S(1)} %get-tuple-element.134), channel_id=1, source_target_pairs={{0,16},{16,32},{32,48},{48,64},{64,80},{80,96},{96,112},{112,128},... | collective-permute-start | bytes 6152 | tf_op jit(solution)/shard_map/ppermute | solution.py:20
  66.0 7.9 %collective-permute-start.6 = (f32[4,1,128]{2,1,0:T(1,128)S(1)}, f32[4,1,128]{2,1,0:T(1,128)S(1)}, u32[]{:S(2)}, u32[]{:S(2)}) collective-permute-start(f32[4,1,128]{2,1,0:T(1,128)S(1)} %get-tuple-element.120), channel_id=1, source_target_pairs={{0,1},{1,2},{2,3},{3,4},{4,5},{5,6},{6,7},{7,8},{8,9},{9,10},{10,1... | collective-permute-start | bytes 6152 | tf_op jit(solution)/shard_map/ppermute | solution.py:20
  72.0 4.9 %collective-permute-start.7 = (f32[4,1,128]{2,1,0:T(1,128)S(1)}, f32[4,1,128]{2,1,0:T(1,128)S(1)}, u32[]{:S(2)}, u32[]{:S(2)}) collective-permute-start(f32[4,1,128]{2,1,0:T(1,128)S(1)} %get-tuple-element.119), channel_id=1, source_target_pairs={{1,0},{2,1},{3,2},{4,3},{5,4},{6,5},{7,6},{8,7},{9,8},{10,9},{11,1... | collective-permute-start | bytes 6152 | tf_op jit(solution)/shard_map/ppermute | solution.py:22
  83.1 15.8 %all-to-all-start.2 = ((f32[64,1,2]{2,1,0:T(1,128)}), f32[64,1,2]{2,1,0:T(1,128)S(1)}, u32[]{:S(2)}, u32[]{:S(2)}) async-start(f32[64,1,2]{2,1,0:T(1,128)} %broadcast_in_dim.22), calls=%async_computation.2 | async-start | bytes 65536 | tf_op jit(solution)/shard_map/all_to_all | solution.py:31
  110.1 5.3 %collective-permute-start.9 = (f32[1,4,128]{2,1,0:T(4,128)S(1)}, f32[1,4,128]{2,1,0:T(4,128)S(1)}, u32[]{:S(2)}, u32[]{:S(2)}) collective-permute-start(f32[1,4,128]{2,1,0:T(4,128)S(1)} %get-tuple-element.133), channel_id=1, source_target_pairs={{16,0},{32,16},{48,32},{64,48},{80,64},{96,80},{112,96},{128,112},... | collective-permute-start | bytes 6152 | tf_op jit(solution)/shard_map/ppermute | solution.py:22
  111.4 4.7 %collective-permute-start.8 = (f32[1,4,128]{2,1,0:T(4,128)S(1)}, f32[1,4,128]{2,1,0:T(4,128)S(1)}, u32[]{:S(2)}, u32[]{:S(2)}) collective-permute-start(f32[1,4,128]{2,1,0:T(4,128)S(1)} %get-tuple-element.132), channel_id=1, source_target_pairs={{0,16},{16,32},{32,48},{48,64},{64,80},{80,96},{96,112},{112,128},... | collective-permute-start | bytes 6152 | tf_op jit(solution)/shard_map/ppermute | solution.py:20
  116.1 7.3 %collective-permute-start.10 = (f32[4,1,128]{2,1,0:T(1,128)S(1)}, f32[4,1,128]{2,1,0:T(1,128)S(1)}, u32[]{:S(2)}, u32[]{:S(2)}) collective-permute-start(f32[4,1,128]{2,1,0:T(1,128)S(1)} %get-tuple-element.118), channel_id=1, source_target_pairs={{0,1},{1,2},{2,3},{3,4},{4,5},{5,6},{6,7},{7,8},{8,9},{9,10},{10,1... | collective-permute-start | bytes 6152 | tf_op jit(solution)/shard_map/ppermute | solution.py:20
  121.5 4.9 %collective-permute-start.11 = (f32[4,1,128]{2,1,0:T(1,128)S(1)}, f32[4,1,128]{2,1,0:T(1,128)S(1)}, u32[]{:S(2)}, u32[]{:S(2)}) collective-permute-start(f32[4,1,128]{2,1,0:T(1,128)S(1)} %get-tuple-element.117), channel_id=1, source_target_pairs={{1,0},{2,1},{3,2},{4,3},{5,4},{6,5},{7,6},{8,7},{9,8},{10,9},{11,1... | collective-permute-start | bytes 6152 | tf_op jit(solution)/shard_map/ppermute | solution.py:22
  131.6 15.8 %all-to-all-start.4 = ((f32[64,1,3]{2,1,0:T(1,128)}), f32[64,1,3]{2,1,0:T(1,128)S(1)}, u32[]{:S(2)}, u32[]{:S(2)}) async-start(f32[64,1,3]{2,1,0:T(1,128)} %broadcast_in_dim.24), calls=%async_computation.4 | async-start | bytes 65536 | tf_op jit(solution)/shard_map/all_to_all | solution.py:31
  158.2 5.3 %collective-permute-start.13 = (f32[1,4,128]{2,1,0:T(4,128)S(1)}, f32[1,4,128]{2,1,0:T(4,128)S(1)}, u32[]{:S(2)}, u32[]{:S(2)}) collective-permute-start(f32[1,4,128]{2,1,0:T(4,128)S(1)} %get-tuple-element.131), channel_id=1, source_target_pairs={{16,0},{32,16},{48,32},{64,48},{80,64},{96,80},{112,96},{128,112},... | collective-permute-start | bytes 6152 | tf_op jit(solution)/shard_map/ppermute | solution.py:22
  159.5 4.7 %collective-permute-start.12 = (f32[1,4,128]{2,1,0:T(4,128)S(1)}, f32[1,4,128]{2,1,0:T(4,128)S(1)}, u32[]{:S(2)}, u32[]{:S(2)}) collective-permute-start(f32[1,4,128]{2,1,0:T(4,128)S(1)} %get-tuple-element.130), channel_id=1, source_target_pairs={{0,16},{16,32},{32,48},{48,64},{64,80},{80,96},{96,112},{112,128},... | collective-permute-start | bytes 6152 | tf_op jit(solution)/shard_map/ppermute | solution.py:20
  164.2 7.3 %collective-permute-start.14 = (f32[4,1,128]{2,1,0:T(1,128)S(1)}, f32[4,1,128]{2,1,0:T(1,128)S(1)}, u32[]{:S(2)}, u32[]{:S(2)}) collective-permute-start(f32[4,1,128]{2,1,0:T(1,128)S(1)} %get-tuple-element.116), channel_id=1, source_target_pairs={{0,1},{1,2},{2,3},{3,4},{4,5},{5,6},{6,7},{7,8},{8,9},{9,10},{10,1... | collective-permute-start | bytes 6152 | tf_op jit(solution)/shard_map/ppermute | solution.py:20
  169.6 4.9 %collective-permute-start.15 = (f32[4,1,128]{2,1,0:T(1,128)S(1)}, f32[4,1,128]{2,1,0:T(1,128)S(1)}, u32[]{:S(2)}, u32[]{:S(2)}) collective-permute-start(f32[4,1,128]{2,1,0:T(1,128)S(1)} %get-tuple-element.115), channel_id=1, source_target_pairs={{1,0},{2,1},{3,2},{4,3},{5,4},{6,5},{7,6},{8,7},{9,8},{10,9},{11,1... | collective-permute-start | bytes 6152 | tf_op jit(solution)/shard_map/ppermute | solution.py:22
  174.8 103.4 %copy-start.1 = (f32[2,4,128]{2,1,0:T(4,128)S(1)}, f32[2,4,128]{2,1,0:T(4,128)}, u32[]{:S(2)}) copy-start(f32[2,4,128]{2,1,0:T(4,128)} %param.25) | copy-start | bytes 12292
  179.8 15.8 %all-to-all-start.6 = ((f32[64,1,4]{2,1,0:T(1,128)}), f32[64,1,4]{2,1,0:T(1,128)S(1)}, u32[]{:S(2)}, u32[]{:S(2)}) async-start(f32[64,1,4]{2,1,0:T(1,128)} %broadcast_in_dim.26), calls=%async_computation.6 | async-start | bytes 65536 | tf_op jit(solution)/shard_map/all_to_all | solution.py:31
  206.2 8.7 %collective-permute-start.17 = (f32[1,4,128]{2,1,0:T(4,128)S(1)}, f32[1,4,128]{2,1,0:T(4,128)S(1)}, u32[]{:S(2)}, u32[]{:S(2)}) collective-permute-start(f32[1,4,128]{2,1,0:T(4,128)S(1)} %get-tuple-element.129), channel_id=1, source_target_pairs={{16,0},{32,16},{48,32},{64,48},{80,64},{96,80},{112,96},{128,112},... | collective-permute-start | bytes 6152 | tf_op jit(solution)/shard_map/ppermute | solution.py:22
  207.5 7.4 %collective-permute-start.16 = (f32[1,4,128]{2,1,0:T(4,128)S(1)}, f32[1,4,128]{2,1,0:T(4,128)S(1)}, u32[]{:S(2)}, u32[]{:S(2)}) collective-permute-start(f32[1,4,128]{2,1,0:T(4,128)S(1)} %get-tuple-element.128), channel_id=1, source_target_pairs={{0,16},{16,32},{32,48},{48,64},{64,80},{80,96},{96,112},{112,128},... | collective-permute-start | bytes 6152 | tf_op jit(solution)/shard_map/ppermute | solution.py:20
  215.0 6.7 %collective-permute-start.18 = (f32[4,1,128]{2,1,0:T(1,128)S(1)}, f32[4,1,128]{2,1,0:T(1,128)S(1)}, u32[]{:S(2)}, u32[]{:S(2)}) collective-permute-start(f32[4,1,128]{2,1,0:T(1,128)S(1)} %get-tuple-element.114), channel_id=1, source_target_pairs={{0,1},{1,2},{2,3},{3,4},{4,5},{5,6},{6,7},{7,8},{8,9},{9,10},{10,1... | collective-permute-start | bytes 6152 | tf_op jit(solution)/shard_map/ppermute | solution.py:20
  219.8 4.9 %collective-permute-start.19 = (f32[4,1,128]{2,1,0:T(1,128)S(1)}, f32[4,1,128]{2,1,0:T(1,128)S(1)}, u32[]{:S(2)}, u32[]{:S(2)}) collective-permute-start(f32[4,1,128]{2,1,0:T(1,128)S(1)} %get-tuple-element.113), channel_id=1, source_target_pairs={{1,0},{2,1},{3,2},{4,3},{5,4},{6,5},{7,6},{8,7},{9,8},{10,9},{11,1... | collective-permute-start | bytes 6152 | tf_op jit(solution)/shard_map/ppermute | solution.py:22
  229.9 15.8 %all-to-all-start.8 = ((f32[64,1,5]{2,1,0:T(1,128)}), f32[64,1,5]{2,1,0:T(1,128)S(1)}, u32[]{:S(2)}, u32[]{:S(2)}) async-start(f32[64,1,5]{2,1,0:T(1,128)} %broadcast_in_dim.28), calls=%async_computation.8 | async-start | bytes 65536 | tf_op jit(solution)/shard_map/all_to_all | solution.py:31
  246.4 7.3 %all-to-all-start.9 = ((f32[4,1,5]{2,1,0:T(1,128)}), f32[4,1,5]{2,1,0:T(1,128)S(1)}, u32[]{:S(2)}, u32[]{:S(2)}) async-start(f32[4,1,5]{2,1,0:T(1,128)} %broadcast_in_dim.29), calls=%async_computation.9 | async-start | bytes 4096 | tf_op jit(solution)/shard_map/all_to_all | solution.py:31
  (1 other events, 19.2 us)
where the time goes:
time: 281 us; the launch traced here: 279 us
  starting transfers between devices  107 us (38%)
  waiting for transfers between devices  60 us (21%)
  blocking collectives  31.1 us (11%)
  other arithmetic  23.8 us (8%)
  between operations  23.4 us (8%)
  local copies, waits for them, and re-layouts  17.6 us (6%)
  matrix products  16.1 us (6%)
    ppermute x10, starting transfers between devices, extended(): lax.ppermute(tail, axis, [(i, (i + 1) % count) for i in range(ends)])  44.4 us
    all_to_all x6, starting transfers between devices, copy_for_each(): return lax.all_to_all(copies, axis, split_axis=0, concat_axis=0, tiled=True)  44.4 us
    all_to_all x6, waiting for transfers between devices, copy_for_each(): return lax.all_to_all(copies, axis, split_axis=0, concat_axis=0, tiled=True)  43.7 us
    all_to_all x4, blocking collectives, copy_for_each(): return lax.all_to_all(copies, axis, split_axis=0, concat_axis=0, tiled=True)  31.1 us
    ppermute x10, starting transfers between devices, extended(): lax.ppermute(head, axis, [((i + 1) % count, i) for i in range(ends)])  18.1 us
    ppermute x10, waiting for transfers between devices, extended(): lax.ppermute(head, axis, [((i + 1) % count, i) for i in range(ends)])  14.8 us
    dot_general x5, matrix products, operate(): jnp.einsum('xyskl,xysl->xyk', matrix_tiles, picked, precision=lax.Precisi...  13.4 us
    another operation x8, other arithmetic  7.88 us
  transfers between devices with their start and end apart: 26, of which 13 were waited for; matrix products, arithmetic and copies ran while one was open for 4% of the time, Pallas kernels for 0%

commit v1 on v0

v1 whole, which is shorter than its diff:
```python
import functools

import jax
import jax.numpy as jnp
from jax import lax
from jax.experimental import pallas as pl
from jax.experimental.pallas import tpu as pltpu
from jax.sharding import PartitionSpec as P

ITERS = 4
SLOTS = 6
BLK = 128
RBX = 2
RBY = 4
ROWS = RBX * RBY
SHIFT = 3.0
SCALE = 0.25
PAIRS = [(i, j) for j in range(ITERS + 1) for i in range(j + 1)]
MESH = pl.DeviceIdType.MESH

UP, DOWN, LEFT, RIGHT = (0, 4, -1, 0), (4, 4, 1, 0), (8, 2, 0, -1), (10, 2, 0, 1)
CORNERS = ((12, 1, -1, -1), (13, 1, -1, 1), (14, 1, 1, -1), (15, 1, 1, 1))
SIDES = (UP, DOWN, LEFT, RIGHT, *CORNERS)
GRID_OF = (
    [(0, 1 + j) for j in range(RBY)]
    + [(3, 1 + j) for j in range(RBY)]
    + [(1 + i, 0) for i in range(RBX)]
    + [(1 + i, 5) for i in range(RBX)]
    + [(0, 0), (0, 5), (3, 0), (3, 5)]
)
ZERO_ROW = 24


def kernel(
    nx, ny,
    tiles_hbm, codes, counts, right_hbm, guess_hbm,
    solution_ref, residual_ref, hessenberg_ref,
    tiles, grid, where, sent, landed, basis, guess, right,
    gram_rows, gram, line, sums_x, sums_y,
    tile_sems, load_sems, send_sems, recv_sems, sum_send_sems, sum_recv_sems,
):
    gx, gy = lax.axis_index("gx"), lax.axis_index("gy")

    loads = [
        pltpu.make_async_copy(guess_hbm, guess, load_sems.at[0]),
        pltpu.make_async_copy(right_hbm, right, load_sems.at[1]),
    ]
    loads[0].start()
    loads[1].start()
    order = [(i, j) for j in (1, 2) for i in (0, 1)] + [(i, j) for j in (0, 3) for i in (0, 1)]
    tile_loads = {
        (i, j): pltpu.make_async_copy(tiles_hbm.at[i, j], tiles.at[i, j], tile_sems.at[i * RBY + j])
        for i, j in order
    }
    for at in order:
        tile_loads[at].start()

    zero_line = jnp.zeros((1, BLK), jnp.float32)
    for step in range(ITERS + 1):
        for row in range(16):
            landed[step, row] = zero_line
    grid[ZERO_ROW] = zero_line

    def exists(side):
        _, _, dx, dy = side
        ok = None
        for at, d, n in ((gx, dx, nx), (gy, dy, ny)):
            if d:
                here = at > 0 if d < 0 else at < n - 1
                ok = here if ok is None else jnp.logical_and(ok, here)
        return ok

    barrier = pltpu.get_barrier_semaphore()

    def greet(d, _):
        pl.semaphore_signal(
            barrier, inc=1, device_id={"gx": lax.rem(gx + d, nx), "gy": gy}, device_id_type=MESH
        )
        return 0

    def greet_y(d, _):
        pl.semaphore_signal(
            barrier, inc=1, device_id={"gx": gx, "gy": lax.rem(gy + d, ny)}, device_id_type=MESH
        )
        return 0

    awaited = jnp.int32(nx - 1 + ny - 1)
    for side in CORNERS:
        there = exists(side)

        @pl.when(there)
        def _():
            pl.semaphore_signal(
                barrier, inc=1, device_id={"gx": gx + side[2], "gy": gy + side[3]}, device_id_type=MESH
            )

        awaited = awaited + jnp.where(there, 1, 0)
    lax.fori_loop(1, nx, greet, 0)
    lax.fori_loop(1, ny, greet_y, 0)

    for i in range(RBX):
        for j in range(RBY):
            live = counts[i, j]
            for s in range(1, SLOTS):
                code = codes[i, j, s]
                down = jnp.where(code >= 3, 1, 0) + jnp.where(code >= 6, 1, 0)
                row = (i + down) * 6 + j + code - 3 * down
                where[(i * RBY + j) * SLOTS + s] = jnp.where(s < live, row, ZERO_ROW)

    loads[0].wait()
    for i in range(RBX):
        for j in range(RBY):
            b = i * RBY + j
            row = guess[b : b + 1, :]
            sent[0, i, j] = row
            grid[(1 + i) * 6 + 1 + j] = row

    def transfer(step, side, source, target):
        index = SIDES.index(side)
        return pltpu.make_async_remote_copy(
            src_ref=source,
            dst_ref=target,
            send_sem=send_sems.at[step, index],
            recv_sem=recv_sems.at[step, index],
            device_id={"gx": gx - side[2], "gy": gy - side[3]},
            device_id_type=MESH,
        )

    def pieces(step, side):
        first, rows, dx, dy = side
        i = 1 if dx < 0 else 0
        j = RBY - 1 if dy < 0 else 0
        if dx and dy:
            return [transfer(step, side, sent.at[step, i, pl.ds(j, 1)], landed.at[step, pl.ds(first, 1)])]
        if dx:
            return [transfer(step, side, sent.at[step, i], landed.at[step, pl.ds(first, rows)])]
        return [
            transfer(step, side, sent.at[step, r, pl.ds(j, 1)], landed.at[step, pl.ds(first + r, 1)])
            for r in range(RBX)
        ]

    def whole(step, side):
        first, rows, _, _ = side
        part = landed.at[step, pl.ds(first, rows)]
        return transfer(step, side, part, part)

    def opposite(side):
        return (side[0], side[1], -side[2], -side[3])

    def send(step):
        for side in (*CORNERS, UP, DOWN, LEFT, RIGHT):

            @pl.when(exists(opposite(side)))
            def _():
                for piece in pieces(step, side):
                    piece.start()

    def receive(step, sides):
        for side in sides:

            @pl.when(exists(side))
            def _():
                whole(step, side).wait_recv()

        for side in sides:
            for row in range(side[0], side[0] + side[1]):
                r, c = GRID_OF[row]
                grid[r * 6 + c] = landed[step, row]

    def product(i, j):
        total = None
        for s in range(SLOTS):
            at = (1 + i) * 6 + 1 + j if s == 0 else where[(i * RBY + j) * SLOTS + s]
            term = tiles[i, j, s] * grid[at]
            total = term if total is None else total + term
        return jnp.sum(total.T, axis=0, keepdims=True)

    def advance(step, blocks):
        fresh = []
        for i, j in blocks:
            b = i * RBY + j
            image = product(i, j)
            if step == 0:
                new = right[b : b + 1, :] - image
            else:
                new = SCALE * (image - SHIFT * basis[step - 1, b : b + 1, :])
            fresh.append(new)
        for (i, j), new in zip(blocks, fresh):
            b = i * RBY + j
            basis[step, b : b + 1, :] = new
            if step < ITERS:
                sent[step + 1, i, j] = new

    def multiply_pairs(column):
        last = basis[column]
        for index, (i, j) in enumerate(PAIRS):
            if j == column:
                gram_rows[index : index + 1, :] = jnp.sum(basis[i] * last, axis=0, keepdims=True)

    gram_rows[len(PAIRS) : 16, :] = zero_line
    pl.semaphore_wait(barrier, awaited)
    send(0)
    loads[1].wait()
    for step in range(ITERS + 1):
        if step:
            multiply_pairs(step - 1)
            for i in range(RBX):
                for j in range(RBY):
                    grid[(1 + i) * 6 + 1 + j] = sent[step, i, j]
        for blocks, sides in ((order[:4], (UP, DOWN)), (order[4:], (LEFT, RIGHT, *CORNERS))):
            if step == 0:
                for at in blocks:
                    tile_loads[at].wait()
            receive(step, sides)
            advance(step, blocks)
        if step < ITERS:
            send(step + 1)
    multiply_pairs(ITERS)

    sublane = lax.broadcasted_iota(jnp.int32, (16, BLK), 0)
    lane = lax.broadcasted_iota(jnp.int32, (16, BLK), 1)
    own = sublane == lane

    total = jnp.sum(gram_rows[...], axis=1, keepdims=True)
    total = jnp.sum(jnp.where(own, jnp.broadcast_to(total, (16, BLK)), 0.0), axis=0, keepdims=True)
    for stage, (axis, n, here, sums) in enumerate((("gx", nx, gx, sums_x), ("gy", ny, gy, sums_y))):
        line[stage] = total
        sums[here] = total

        def copy_to(d):
            there = {"gx": gx, "gy": gy}
            there[axis] = lax.rem(here + d, n)
            return pltpu.make_async_remote_copy(
                src_ref=line.at[pl.ds(stage, 1)],
                dst_ref=sums.at[pl.ds(here, 1)],
                send_sem=sum_send_sems.at[stage],
                recv_sem=sum_recv_sems.at[stage],
                device_id=there,
                device_id_type=MESH,
            )

        for d in range(1, n):
            copy_to(d).start()
        others = sums.at[pl.ds(0, n - 1)]
        pltpu.make_async_remote_copy(
            src_ref=others,
            dst_ref=others,
            send_sem=sum_send_sems.at[stage],
            recv_sem=sum_recv_sems.at[stage],
            device_id={"gx": gx, "gy": gy},
            device_id_type=MESH,
        ).wait()
        parts = [sums[d] for d in range(n)]
        while len(parts) > 1:
            parts = [parts[k] + parts[k + 1] for k in range(0, len(parts), 2)]
        total = parts[0]
    spread = jnp.sum(
        jnp.where(own, jnp.broadcast_to(total, (16, BLK)), 0.0), axis=1, keepdims=True
    )
    gram[...] = jnp.broadcast_to(spread, (16, BLK))
    g = {}
    for index, (i, j) in enumerate(PAIRS):
        g[i, j] = jnp.broadcast_to(gram[index : index + 1, :], (ROWS, BLK))

    def factor(m, n):
        r, inverse = {}, []
        m = dict(m)
        for k in range(n):
            root = jnp.sqrt(m[k, k])
            r[k, k] = root
            inverse.append(1.0 / root)
            for j in range(k + 1, n):
                r[k, j] = m[k, j] * inverse[k]
            for i in range(k + 1, n):
                for j in range(i, n):
                    m[i, j] = m[i, j] - r[k, i] * r[k, j]
        return r, inverse

    r, inverse = factor(g, ITERS + 1)
    h = {}
    for k in range(ITERS):
        for i in range(k + 2):
            value = r[i, k + 1]
            for m in range(max(i - 1, 0), k):
                value = value - h[i, m] * r[m, k]
            h[i, k] = value * inverse[k]
    for i, k in h:
        h[i, k] = h[i, k] * (1.0 / SCALE)
        if i == k:
            h[i, k] = h[i, k] + SHIFT
    normal = {}
    for i in range(ITERS):
        for j in range(i, ITERS):
            value = None
            for k in range(i + 2):
                term = h[k, i] * h[k, j]
                value = term if value is None else value + term
            normal[i, j] = value
    target = [r[0, 0] * h[0, k] for k in range(ITERS)]
    lower, scale = factor(normal, ITERS)

    def substitute_back(upper, reciprocal, values):
        found = [None] * ITERS
        for row in reversed(range(ITERS)):
            value = values[row]
            for column in range(row + 1, ITERS):
                value = value - upper[row, column] * found[column]
            found[row] = value * reciprocal[row]
        return found

    forward = []
    for row in range(ITERS):
        value = target[row]
        for column in range(row):
            value = value - lower[column, row] * forward[column]
        forward.append(value * scale[row])
    y = substitute_back(lower, scale, forward)
    weights = substitute_back(r, inverse, y)

    found = guess[...]
    left = basis[0]
    for k in range(ITERS):
        found = found + weights[k] * basis[k]
        left = left - weights[k] * ((1.0 / SCALE) * basis[k + 1] + SHIFT * basis[k])
    solution_ref[...] = found
    residual_ref[...] = left
    sublane, lane = sublane[:ROWS], lane[:ROWS]
    shown = jnp.zeros((ROWS, BLK), jnp.float32)
    for i, k in h:
        shown = jnp.where(jnp.logical_and(sublane == i, lane == k), h[i, k], shown)
    hessenberg_ref[...] = shown[: ITERS + 1, :ITERS]

    for step in range(ITERS + 1):
        for side in SIDES:

            @pl.when(exists(opposite(side)))
            def _():
                whole(step, side).wait_send()


def solution(mesh):
    nx, ny = mesh.shape["gx"], mesh.shape["gy"]

    def body(matrix_tiles, tile_codes, tile_counts, right_side, initial_guess):
        flat = jax.ShapeDtypeStruct((ROWS, BLK), jnp.float32)
        any_space = pl.BlockSpec(memory_space=pl.ANY)
        vmem = pl.BlockSpec(memory_space=pltpu.VMEM)
        smem = pl.BlockSpec(memory_space=pltpu.SMEM)
        found, left, hessenberg = pl.pallas_call(
            functools.partial(kernel, nx, ny),
            out_shape=(flat, flat, jax.ShapeDtypeStruct((ITERS + 1, ITERS), jnp.float32)),
            in_specs=[any_space, smem, smem, any_space, any_space],
            out_specs=(vmem, vmem, vmem),
            scratch_shapes=[
                pltpu.VMEM((RBX, RBY, SLOTS, BLK, BLK), jnp.float32),
                pltpu.VMEM((ZERO_ROW + 1, 1, BLK), jnp.float32),
                pltpu.SMEM((ROWS * SLOTS,), jnp.int32),
                pltpu.VMEM((ITERS + 1, RBX, RBY, 1, BLK), jnp.float32),
                pltpu.VMEM((ITERS + 1, 16, 1, BLK), jnp.float32),
                pltpu.VMEM((ITERS + 1, ROWS, BLK), jnp.float32),
                pltpu.VMEM((ROWS, BLK), jnp.float32),
                pltpu.VMEM((ROWS, BLK), jnp.float32),
                pltpu.VMEM((16, BLK), jnp.float32),
                pltpu.VMEM((16, BLK), jnp.float32),
                pltpu.VMEM((2, 1, BLK), jnp.float32),
                pltpu.VMEM((nx, 1, BLK), jnp.float32),
                pltpu.VMEM((ny, 1, BLK), jnp.float32),
                pltpu.SemaphoreType.DMA((ROWS,)),
                pltpu.SemaphoreType.DMA((2,)),
                pltpu.SemaphoreType.DMA((ITERS + 1, len(SIDES))),
                pltpu.SemaphoreType.DMA((ITERS + 1, len(SIDES))),
                pltpu.SemaphoreType.DMA((2,)),
                pltpu.SemaphoreType.DMA((2,)),
            ],
            compiler_params=pltpu.CompilerParams(collective_id=0, has_side_effects=True),
        )(
            matrix_tiles,
            tile_codes,
            tile_counts,
            right_side.reshape(ROWS, BLK),
            initial_guess.reshape(ROWS, BLK),
        )
        shape = (RBX, RBY, BLK)
        return found.reshape(shape), left.reshape(shape), hessenberg

    split = P("gx", "gy", None)
    return jax.shard_map(
        body,
        mesh=mesh,
        in_specs=(P("gx", "gy", None, None, None), split, P("gx", "gy"), split, split),
        out_specs=(split, split, P()),
        check_vma=False,
    )
```

time: 281 us -> 49.3 us (0.18)
  starting transfers between devices: 107 us -> 0 us
  waiting for transfers between devices: 60 us -> 0 us
  Pallas kernels: 0 us -> 44.5 us
  blocking collectives: 31.1 us -> 0 us
  other arithmetic: 23.8 us -> 0 us
  between operations: 23.4 us -> 0.64 us
  matrix products: 16.1 us -> 0 us
  local copies, waits for them, and re-layouts: 17.6 us -> 3.86 us
    ppermute x20 -> x0, starting transfers between devices: 62.5 us -> none  [the longest x10 44.4 us: extended(): lax.ppermute(tail, axis, [(i, (i + 1) % count) for i in range(ends)])]
    pallas_call x0 -> x1, Pallas kernels: none -> 44.5 us  [body(): pl.pallas_call(functools.partial(kernel, nx, ny), out_shape=(flat, flat,...]
    all_to_all x6 -> x0, starting transfers between devices: 44.4 us -> none  [copy_for_each(): return lax.all_to_all(copies, axis, split_axis=0, concat_axis=0, tiled=True)]
    all_to_all x6 -> x0, waiting for transfers between devices: 43.7 us -> none  [copy_for_each(): return lax.all_to_all(copies, axis, split_axis=0, concat_axis=0, tiled=True)]
    all_to_all x4 -> x0, blocking collectives: 31.1 us -> none  [copy_for_each(): return lax.all_to_all(copies, axis, split_axis=0, concat_axis=0, tiled=True)]
    ppermute x20 -> x0, waiting for transfers between devices: 16.2 us -> none  [the longest x10 14.8 us: extended(): lax.ppermute(head, axis, [((i + 1) % count, i) for i in range(ends)])]
    dot_general x16 -> x0, matrix products: 16.1 us -> none  [the longest x5 13.4 us: operate(): jnp.einsum('xyskl,xysl->xyk', matrix_tiles, picked, precision=lax.Precisi...]
    another operation x18 -> x0, other arithmetic: 9.01 us -> none
  transfers between devices with their start and end apart: 26 -> 0, of which waited for: 13 -> 0; matrix products, arithmetic and copies ran while one was open for 4% -> 0% of each run, Pallas kernels for 0% -> 0%
where the time goes in v1:
time: 49.3 us; the launch traced here: 49 us
  Pallas kernels  44.5 us (90%)
  local copies, waits for them, and re-layouts  3.86 us (8%)
  between operations  0.64 us (1%)
    pallas_call x1, Pallas kernels, body(): pl.pallas_call(functools.partial(kernel, nx, ny), out_shape=(flat, flat,...  44.5 us
    unnamed x3, local copies, waits for them, and re-layouts  3.86 us

profile of v1, /device:TPU:1, one launch (start us, length us, event | category | flops | bytes accessed | tf_op | source)
XLA Modules:
  0.0 49.0 jit_solution(18042691031758694444)
XLA Ops:
  0.6 44.5 %shard_map.76 = (f32[8,128]{1,0:T(8,128)}, f32[8,128]{1,0:T(8,128)}, f32[5,4]{1,0:T(8,128)}) custom-call(f32[2,4,6,128,128]{4,3,2,1,0:T(8,128)} %tiles_hbm.1, s32[2,4,6]{2,1,0:T(4,128)} %codes.1, s32[2,4]{1,0:T(2,128)} %counts.1, f32[8,128]{1,0:T(8,128)} %bitcast.4, f32[8,128]{1,0:T(8,128)} %bitcast.5), custom_call_target="tpu_custom_call" | custom-call | tf_op jit(solution)/shard_map/pallas_call | solution.py:349
  45.2 1.3 %copy.8 = f32[5,4]{0,1:T(4,128)} copy(f32[5,4]{1,0:T(8,128)} %get-tuple-element.11) | data formatting | bytes 160
  46.5 1.3 %copy.11 = f32[2,4,128]{2,1,0:T(4,128)} copy(f32[2,4,128]{2,1,0:T(4,128)} %bitcast.7) | data formatting | bytes 8192
  47.8 1.3 %copy.12 = f32[2,4,128]{2,1,0:T(4,128)} copy(f32[2,4,128]{2,1,0:T(4,128)} %bitcast.6) | data formatting | bytes 8192

commit v2 on v1

--- a/solution.py
+++ b/solution.py
@@ -29,31 +29,18 @@
     + [(0, 0), (0, 5), (3, 0), (3, 5)]
 )
 ZERO_ROW = 24
+VMEM_BYTES = 67043328
 
 
 def kernel(
     nx, ny,
-    tiles_hbm, codes, counts, right_hbm, guess_hbm,
-    solution_ref, residual_ref, hessenberg_ref,
-    tiles, grid, where, sent, landed, basis, guess, right,
-    gram_rows, gram, line, sums_x, sums_y,
+    tiles_hbm, codes_hbm, counts_hbm, right_hbm, guess_hbm,
+    basis, guess, gram,
+    tiles, grid, codes, counts, where, sent, landed, right,
+    gram_rows, line, sums_x, sums_y,
     tile_sems, load_sems, send_sems, recv_sems, sum_send_sems, sum_recv_sems,
 ):
     gx, gy = lax.axis_index("gx"), lax.axis_index("gy")
-
-    loads = [
-        pltpu.make_async_copy(guess_hbm, guess, load_sems.at[0]),
-        pltpu.make_async_copy(right_hbm, right, load_sems.at[1]),
-    ]
-    loads[0].start()
-    loads[1].start()
-    order = [(i, j) for j in (1, 2) for i in (0, 1)] + [(i, j) for j in (0, 3) for i in (0, 1)]
-    tile_loads = {
-        (i, j): pltpu.make_async_copy(tiles_hbm.at[i, j], tiles.at[i, j], tile_sems.at[i * RBY + j])
-        for i, j in order
-    }
-    for at in order:
-        tile_loads[at].start()
 
     zero_line = jnp.zeros((1, BLK), jnp.float32)
     for step in range(ITERS + 1):
@@ -98,14 +85,21 @@
     lax.fori_loop(1, nx, greet, 0)
     lax.fori_loop(1, ny, greet_y, 0)
 
-    for i in range(RBX):
-        for j in range(RBY):
-            live = counts[i, j]
-            for s in range(1, SLOTS):
-                code = codes[i, j, s]
-                down = jnp.where(code >= 3, 1, 0) + jnp.where(code >= 6, 1, 0)
-                row = (i + down) * 6 + j + code - 3 * down
-                where[(i * RBY + j) * SLOTS + s] = jnp.where(s < live, row, ZERO_ROW)
+    loads = [
+        pltpu.make_async_copy(guess_hbm, guess, load_sems.at[0]),
+        pltpu.make_async_copy(right_hbm, right, load_sems.at[1]),
+        pltpu.make_async_copy(codes_hbm, codes, load_sems.at[2]),
+        pltpu.make_async_copy(counts_hbm, counts, load_sems.at[3]),
+    ]
+    for load in loads:
+        load.start()
+    order = [(i, j) for j in (1, 2) for i in (0, 1)] + [(i, j) for j in (0, 3) for i in (0, 1)]
+    tile_loads = {
+        (i, j): pltpu.make_async_copy(tiles_hbm.at[i, j], tiles.at[i, j], tile_sems.at[i * RBY + j])
+        for i, j in order
+    }
+    for at in order:
+        tile_loads[at].start()
 
     loads[0].wait()
     for i in range(RBX):
@@ -200,6 +194,17 @@
     gram_rows[len(PAIRS) : 16, :] = zero_line
     pl.semaphore_wait(barrier, awaited)
     send(0)
+    loads[2].wait()
+    loads[3].wait()
+    for i in range(RBX):
+        for j in range(RBY):
+            live = counts[i, j]
+            for s in range(1, SLOTS):
+                code = codes[i, j, s]
+                down = jnp.where(code >= 3, 1, 0) + jnp.where(code >= 6, 1, 0)
+                row = (i + down) * 6 + j + code - 3 * down
+                where[(i * RBY + j) * SLOTS + s] = jnp.where(s < live, row, ZERO_ROW)
+
     loads[1].wait()
     for step in range(ITERS + 1):
         if step:
@@ -254,13 +259,27 @@
         while len(parts) > 1:
             parts = [parts[k] + parts[k + 1] for k in range(0, len(parts), 2)]
         total = parts[0]
+    gram[...] = total
+
+    for step in range(ITERS + 1):
+        for side in SIDES:
+
+            @pl.when(exists(opposite(side)))
+            def _():
+                whole(step, side).wait_send()
+
+
+def finish(basis, guess, gram, solution_ref, residual_ref, hessenberg_ref, entries):
+    sublane = lax.broadcasted_iota(jnp.int32, (16, BLK), 0)
+    lane = lax.broadcasted_iota(jnp.int32, (16, BLK), 1)
+    own = sublane == lane
     spread = jnp.sum(
-        jnp.where(own, jnp.broadcast_to(total, (16, BLK)), 0.0), axis=1, keepdims=True
+        jnp.where(own, jnp.broadcast_to(gram[...], (16, BLK)), 0.0), axis=1, keepdims=True
     )
-    gram[...] = jnp.broadcast_to(spread, (16, BLK))
+    entries[...] = jnp.broadcast_to(spread, (16, BLK))
     g = {}
     for index, (i, j) in enumerate(PAIRS):
-        g[i, j] = jnp.broadcast_to(gram[index : index + 1, :], (ROWS, BLK))
+        g[i, j] = jnp.broadcast_to(entries[index : index + 1, :], (ROWS, BLK))
 
     def factor(m, n):
         r, inverse = {}, []
@@ -327,15 +346,8 @@
     sublane, lane = sublane[:ROWS], lane[:ROWS]
     shown = jnp.zeros((ROWS, BLK), jnp.float32)
     for i, k in h:
-        shown = jnp.where(jnp.logical_and(sublane == i, lane == k), h[i, k], shown)
-    hessenberg_ref[...] = shown[: ITERS + 1, :ITERS]
-
-    for step in range(ITERS + 1):
-        for side in SIDES:
-
-            @pl.when(exists(opposite(side)))
-            def _():
-                whole(step, side).wait_send()
+        shown = jnp.where(jnp.logical_and(sublane == k, lane == i), h[i, k], shown)
+    hessenberg_ref[...] = shown[:ITERS, : ITERS + 1]
 
 
 def solution(mesh):
@@ -343,36 +355,40 @@
 
     def body(matrix_tiles, tile_codes, tile_counts, right_side, initial_guess):
         flat = jax.ShapeDtypeStruct((ROWS, BLK), jnp.float32)
-        any_space = pl.BlockSpec(memory_space=pl.ANY)
+        hbm = pl.BlockSpec(memory_space=pltpu.HBM)
         vmem = pl.BlockSpec(memory_space=pltpu.VMEM)
-        smem = pl.BlockSpec(memory_space=pltpu.SMEM)
-        found, left, hessenberg = pl.pallas_call(
+        parts = pl.pallas_call(
             functools.partial(kernel, nx, ny),
-            out_shape=(flat, flat, jax.ShapeDtypeStruct((ITERS + 1, ITERS), jnp.float32)),
-            in_specs=[any_space, smem, smem, any_space, any_space],
+            out_shape=(
+                pltpu.VMEM((ITERS + 1, ROWS, BLK), jnp.float32),
+                pltpu.VMEM((ROWS, BLK), jnp.float32),
+                pltpu.VMEM((1, BLK), jnp.float32),
+            ),
+            in_specs=[hbm] * 5,
             out_specs=(vmem, vmem, vmem),
             scratch_shapes=[
                 pltpu.VMEM((RBX, RBY, SLOTS, BLK, BLK), jnp.float32),
                 pltpu.VMEM((ZERO_ROW + 1, 1, BLK), jnp.float32),
+                pltpu.SMEM((RBX, RBY, SLOTS), jnp.int32),
+                pltpu.SMEM((RBX, RBY), jnp.int32),
                 pltpu.SMEM((ROWS * SLOTS,), jnp.int32),
                 pltpu.VMEM((ITERS + 1, RBX, RBY, 1, BLK), jnp.float32),
                 pltpu.VMEM((ITERS + 1, 16, 1, BLK), jnp.float32),
-                pltpu.VMEM((ITERS + 1, ROWS, BLK), jnp.float32),
                 pltpu.VMEM((ROWS, BLK), jnp.float32),
-                pltpu.VMEM((ROWS, BLK), jnp.float32),
-                pltpu.VMEM((16, BLK), jnp.float32),
                 pltpu.VMEM((16, BLK), jnp.float32),
                 pltpu.VMEM((2, 1, BLK), jnp.float32),
                 pltpu.VMEM((nx, 1, BLK), jnp.float32),
                 pltpu.VMEM((ny, 1, BLK), jnp.float32),
                 pltpu.SemaphoreType.DMA((ROWS,)),
-                pltpu.SemaphoreType.DMA((2,)),
+                pltpu.SemaphoreType.DMA((4,)),
                 pltpu.SemaphoreType.DMA((ITERS + 1, len(SIDES))),
                 pltpu.SemaphoreType.DMA((ITERS + 1, len(SIDES))),
                 pltpu.SemaphoreType.DMA((2,)),
                 pltpu.SemaphoreType.DMA((2,)),
             ],
-            compiler_params=pltpu.CompilerParams(collective_id=0, has_side_effects=True),
+            compiler_params=pltpu.CompilerParams(
+                collective_id=0, has_side_effects=True, vmem_limit_bytes=VMEM_BYTES - 40960
+            ),
         )(
             matrix_tiles,
             tile_codes,
@@ -380,8 +396,16 @@
             right_side.reshape(ROWS, BLK),
             initial_guess.reshape(ROWS, BLK),
         )
+        found, left, hessenberg = pl.pallas_call(
+            finish,
+            out_shape=(flat, flat, jax.ShapeDtypeStruct((ITERS, ITERS + 1), jnp.float32)),
+            in_specs=[vmem] * 3,
+            out_specs=(vmem, vmem, vmem),
+            scratch_shapes=[pltpu.VMEM((16, BLK), jnp.float32)],
+            compiler_params=pltpu.CompilerParams(vmem_limit_bytes=1 << 20),
+        )(*parts)
         shape = (RBX, RBY, BLK)
-        return found.reshape(shape), left.reshape(shape), hessenberg
+        return found.reshape(shape), left.reshape(shape), hessenberg.T
 
     split = P("gx", "gy", None)
     return jax.shard_map(

time: 49.3 us -> 44.5 us (0.903)
  local copies, waits for them, and re-layouts: 3.86 us -> 0 us
  Pallas kernels: 44.5 us -> 43.8 us
    unnamed x3 -> x0, local copies, waits for them, and re-layouts: 3.86 us -> none
    pallas_call x1 -> x2, Pallas kernels: 44.5 us -> 43.8 us  [the longest x1 43 us: body(): pl.pallas_call(functools.partial(kernel, nx, ny), out_shape=(pltpu.VMEM((...]
where the time goes in v2:
time: 44.5 us; the launch traced here: 44.4 us
  Pallas kernels  43.8 us (98%)
  between operations  0.64 us (1%)
    pallas_call x1, Pallas kernels, body(): pl.pallas_call(functools.partial(kernel, nx, ny), out_shape=(pltpu.VMEM((...  43 us

profile of v2, /device:TPU:1, one launch (start us, length us, event | category | flops | bytes accessed | tf_op | source)
XLA Modules:
  0.0 44.4 jit_solution(6580727474658791142)
XLA Ops:
  0.6 43.0 %shard_map.76 = (f32[5,8,128]{2,1,0:T(8,128)S(1)}, f32[8,128]{1,0:T(8,128)S(1)}, f32[1,128]{1,0:T(1,128)S(1)}) custom-call(f32[2,4,6,128,128]{4,3,2,1,0:T(8,128)} %tiles_hbm.1, s32[2,4,6]{2,1,0:T(4,128)} %codes_hbm.1, s32[2,4]{1,0:T(2,128)} %counts_hbm.1, f32[8,128]{1,0:T(8,128)} %bitcast.5, f32[8,128]{1,0:T(8,128)} %bitcast.6), custom_call_target="tpu_custom_call" | custom-call | tf_op jit(solution)/shard_map/pallas_call | solution.py:360
  43.6 0.8 %shard_map.77 = (f32[8,128]{1,0:T(8,128)}, f32[8,128]{1,0:T(8,128)}, f32[4,5]{1,0:T(4,128)}) custom-call(f32[5,8,128]{2,1,0:T(8,128)S(1)} %get-tuple-element.9.basis, f32[8,128]{1,0:T(8,128)S(1)} %get-tuple-element.10.guess, f32[1,128]{1,0:T(1,128)S(1)} %get-tuple-element.11.gram), custom_call_target="tpu_custom_call" | custom-call | tf_op jit(solution)/shard_map/pallas_call | solution.py:399
